TPU v7x, 32 devices: a whole 2x2x4 slice. The times are simulated.
32 devices in a mesh: lat: 8 (over z, y), ch: 4 (over x, core).
Axes of the slice: x: 2, y: 2, z: 4, core: 2. Of those that a mesh axis runs over, the one named last changes fastest.
Arguments:
- field: bfloat16 [728, 256, 1440], P('lat', 'ch'), may hold values from -6 to 6
- legendre: bfloat16 [384, 721, 728], P(('lat', 'ch')), may hold values from -0.21875 to 0.21875
- pair_order: int32 [384], replicated, may hold values from 0 to 383, each once
Outputs:
- coeffs: float32 [384, 721, 2, 256], P(('lat', 'ch'))
Inputs may be any that keep to these rules, and one draw needn't show every extreme that they name: `pair_order`: each of 0 to 383 appears once; a value p below 360 gives its bin the orders p and 719 - p, and a bin with a larger value is empty.
All inputs are finite; a program needn't handle non-finite values.
Results may differ from a plain program's by a relative error of at most 0.0037.
Values may be sent and summed in bfloat16 or wider, within the bound.
A program may use at most 256 MiB of HBM per device.

v0:
```python
import math
import jax
import jax.numpy as jnp
from jax import lax
from jax.sharding import PartitionSpec as P

NLAT = 721


def dft_table(points, modes, lon_count):
    turns = points[:, None] * modes[None, :] % lon_count
    angle = turns.astype(jnp.float32) * (2.0 * math.pi / lon_count)
    return jnp.stack([jnp.cos(angle), -jnp.sin(angle)], axis=-1).astype(jnp.bfloat16)


def project(basis_piece, data_rows, boundary, keep_mask):
    products = jnp.einsum(
        "brl,lbn->brn", basis_piece, data_rows, preferred_element_type=jnp.float32
    )
    bin_count, row_count, width_all = products.shape
    products = products.reshape(bin_count, row_count, 2, 2, width_all // 4)
    degree = jnp.arange(row_count, dtype=jnp.int32)
    upper_part = degree[None, :, None, None] < boundary[:, None, None, None]
    chosen = jnp.where(upper_part, products[:, :, 0], products[:, :, 1])
    return chosen * keep_mask[:, None, None, None].astype(jnp.float32)


def per_device(field, legendre, pair_order):
    lat_rows, chan_dev, lon_count = field.shape
    slot_count = pair_order.shape[0]
    lat_count = lax.axis_size("lat")
    group_size = slot_count // lat_count
    max_order = legendre.shape[1] - 1
    keep_all = pair_order < max_order // 2
    first_order = jnp.where(keep_all, pair_order, 0)
    orders = jnp.stack([first_order, max_order - 1 - first_order], axis=1)
    bound_all = max_order - first_order
    rows_global = lax.axis_index("lat") * lat_rows + jnp.arange(lat_rows, dtype=jnp.int32)
    masked = jnp.where((rows_global < NLAT)[:, None, None], field, jnp.zeros_like(field))
    norm_scale = 2.0 * math.pi / lon_count
    points = jnp.arange(lon_count, dtype=jnp.int32)
    dft_basis = dft_table(points, orders.reshape(-1), lon_count).reshape(lon_count, 4 * slot_count)
    fourier = jnp.einsum("ack,kn->anc", masked, dft_basis, preferred_element_type=jnp.float32)
    fourier = (fourier * norm_scale).astype(jnp.bfloat16).reshape(lat_rows, slot_count, 4, chan_dev)
    received = lax.all_to_all(
        fourier.reshape(lat_rows, slot_count, 4 * chan_dev),
        "lat",
        split_axis=1,
        concat_axis=0,
        tiled=True,
    )
    group_start = lax.axis_index("lat") * group_size
    bound_group = lax.dynamic_slice_in_dim(bound_all, group_start, group_size)
    keep_group = lax.dynamic_slice_in_dim(keep_all, group_start, group_size)
    part_sums = project(
        lax.all_gather(legendre, "ch", axis=0, tiled=True), received, bound_group, keep_group
    )
    return lax.all_to_all(part_sums, "ch", split_axis=0, concat_axis=3, tiled=True)


def solution(mesh):
    in_specs = (P("lat", "ch", None), P(("lat", "ch"), None, None), P())
    out_specs = P(("lat", "ch"), None, None, None)
    return jax.shard_map(
        per_device, mesh=mesh, in_specs=in_specs, out_specs=out_specs, check_vma=False
    )
```

profile of v0, /device:TPU:0, one launch (start us, length us, event | category | flops | bytes accessed | tf_op | source)
XLA Modules:
  0.0 950.9 jit_solution(16822089257262218695)
XLA Ops:
  6.5 0.7 all-gather.2.cloned.1.call-update
  7.3 0.7 broadcast_subtract_fusion.1
  8.0 0.1 copy.30
  8.1 0.1 mul.66
  8.3 19.0 %cosine_convert_fusion = (bf16[1440,768,1]{1,0,2:T(8,128)(2,1)S(1)}, bf16[1440,768,1]{1,0,2:T(8,128)(2,1)S(1)}) fusion(s32[768]{0:T(1024)S(1)} %mul.66), kind=kLoop, calls=%fused_computation.18 | loop fusion | flops 13271040 | bytes 4426752 | tf_op jit(solution)/shard_map/convert
  27.3 3.2 pad_maximum_fusion
  30.6 13.2 %copy.31 = bf16[1440,768,2]{0,2,1:T(2,128)(2,1)} copy(bf16[1440,768,2]{1,0,2:T(8,128)(2,1)} %pad_maximum_fusion) | data formatting | bytes 8847360 | tf_op jit(solution)/shard_map/stack | solution.py:13
  43.8 10.9 %convert_element_type.30 = bf16[1440,1536]{0,1:T(8,128)(2,1)} reshape(bf16[1440,768,2]{0,2,1:T(2,128)(2,1)} %copy.31) | data formatting | bytes 8847360 | tf_op jit(solution)/shard_map/convert_element_type | solution.py:13
  54.7 16.6 %broadcast_select_fusion = bf16[91,64,1440]{2,1,0:T(8,128)(2,1)} fusion(bf16[91,64,1440]{2,1,0:T(8,128)(2,1)} %param.3, pred[91]{0:T(512)(128)(4,1)S(1)} %add_compare_fusion), kind=kLoop, calls=%fused_computation.10 | loop fusion | flops 8386560 | bytes 33546332 | tf_op jit(solution)/shard_map/jit(_where)/select_n | solution.py:39
  71.3 49.8 %fusion = bf16[91,1536,64]{1,0,2:T(8,128)(2,1)} fusion(bf16[91,64,1440]{2,1,0:T(8,128)(2,1)} %broadcast_select_fusion, bf16[1440,1536]{0,1:T(8,128)(2,1)S(1)} %copy-done), kind=kOutput, calls=%fused_computation.1 | convolution fusion | flops 25781403648 | bytes 39088128 | tf_op jit(solution)/shard_map/ack,kn->anc/dot_general | solution.py:43
  121.2 31.3 %copy.34 = bf16[91,1536,64]{0,2,1:T(8,128)(2,1)} copy(bf16[91,1536,64]{1,0,2:T(8,128)(2,1)} %fusion) | data formatting | bytes 35782656 | tf_op jit(solution)/shard_map/convert_element_type | solution.py:44
  152.5 28.4 %copy.35 = bf16[91,384,256]{2,0,1:T(8,128)(2,1)} copy(bf16[91,384,256]{0,2,1:T(8,128)(2,1)} %bitcast.33) | data formatting | bytes 35782656 | tf_op jit(solution)/shard_map/reshape;reshape | solution.py:46
  180.9 7.3 all-to-all-start
  188.1 0.1 dynamic_slice.6
  188.2 0.1 dynamic-slice_convert_fusion
  188.3 0.1 iota_compare_fusion
  188.4 408.6 %all-to-all-done = bf16[91,384,256]{2,0,1:T(8,128)(2,1)} async-done(((bf16[91,384,256]{2,0,1:T(8,128)(2,1)}), bf16[91,384,256]{2,0,1:T(8,128)(2,1)}, u32[]{:S(2)}, u32[]{:S(2)}) %all-to-all-start) | async-done | bytes 17891360 | tf_op jit(solution)/shard_map/all_to_all | solution.py:45
  596.9 19.0 %copy.37 = bf16[8,91,48,256]{3,2,1,0:T(8,128)(2,1)} copy(bf16[8,91,48,256]{3,1,2,0:T(8,128)(2,1)} %bitcast.5) | data formatting | bytes 35782656 | tf_op jit(solution)/shard_map/all_to_all | solution.py:45
  615.9 36.0 %fusion.9 = f32[48,721,256]{2,1,0:T(8,128)} fusion(bf16[48,721,728]{2,1,0:T(8,128)(2,1)} %all-gather.2.cloned.1.call-done, bf16[728,48,256]{2,1,0:T(8,128)(2,1)} %bitcast.36), kind=kOutput, calls=%fused_computation.11 | convolution fusion | flops 12899647488 | bytes 103719168 | tf_op jit(solution)/shard_map/brl,lbn->brn/dot_general | solution.py:17
  651.9 36.0 %copy.39 = f32[48,721,256]{1,2,0:T(8,128)} copy(f32[48,721,256]{2,1,0:T(8,128)} %fusion.9) | data formatting | bytes 70877184 | tf_op jit(solution)/shard_map/brl,lbn->brn/dot_general | solution.py:17
  687.9 12.8 %fusion.2 = f32[48,721,2,64]{1,3,2,0:T(8,128)S(1)} fusion(f32[48,721,2,2,64]{1,4,3,2,0:T(8,128)} %bitcast.32, f32[48]{0:T(128)S(1)} %dynamic-slice_convert_fusion, pred[48,721]{1,0:T(8,128)(4,1)S(1)} %iota_compare_fusion), kind=kLoop, calls=%fused_computation.4 | loop fusion | flops 8859648 | bytes 53192688 | tf_op jit(solution)/shard_map/mul | solution.py:25
  700.8 208.6 %all_to_all.36 = f32[48,721,2,64]{1,3,2,0:T(8,128)S(1)} all-to-all(f32[48,721,2,64]{1,3,2,0:T(8,128)S(1)} %fusion.2), channel_id=1, replica_groups=mesh['lat'=8,'ch'=4] {'ch'}, dimensions={0} | all-to-all | bytes 35438592 | tf_op jit(solution)/shard_map/all_to_all | solution.py:58
  909.4 6.9 copy.41
  916.4 27.7 %copy.42 = f32[12,721,2,256]{3,2,1,0:T(2,128)} copy(f32[12,721,2,256]{1,3,2,0:T(8,128)} %bitcast.35) | data formatting | bytes 35438592 | tf_op jit(solution)/shard_map/all_to_all | solution.py:58
  (11 shorter events, 0.0 us)
Async XLA Ops:
  6.5 609.4 %all-gather.2.cloned.1.call-start = ((), (), s32[]{:S(2)}) async-start(), calls=%async_computation.2 | async-start | bytes 67092480 | tf_op jit(solution)/shard_map/all_gather | solution.py:56
  54.7 16.6 %copy-start = (bf16[1440,1536]{0,1:T(8,128)(2,1)S(1)}, bf16[1440,1536]{0,1:T(8,128)(2,1)}, u32[]{:S(2)}) copy-start(bf16[1440,1536]{0,1:T(8,128)(2,1)} %convert_element_type.30) | copy-start | bytes 13271044
  180.9 7.3 copy-start.1
  180.9 416.1 %all-to-all-start = ((bf16[91,384,256]{2,0,1:T(8,128)(2,1)}), bf16[91,384,256]{2,0,1:T(8,128)(2,1)}, u32[]{:S(2)}, u32[]{:S(2)}) async-start(bf16[91,384,256]{2,0,1:T(8,128)(2,1)} %copy.35), calls=%async_computation | async-start | bytes 37748736 | tf_op jit(solution)/shard_map/all_to_all | solution.py:45
Sparse Core Ops, SparseCore 0:
  8.9 320.7 all-gather.1
where the time goes:
time: 955 us; the launch traced here: 951 us
  waiting for transfers between devices  409 us (43%)
  blocking collectives  209 us (22%)
  local copies, waits for them, and re-layouts  174 us (18%)
  matrix products  85.8 us (9%)
  other arithmetic  52.6 us (6%)
  between operations  13.4 us (1%)
    all_to_all x1, waiting for transfers between devices, per_device(): lax.all_to_all(fourier.reshape(lat_rows, slot_count, 4 * chan_dev), 'lat'...  409 us
    all_to_all x1, blocking collectives, per_device(): lax.all_to_all(part_sums, 'ch', split_axis=0, concat_axis=3, tiled=True)  209 us
    dot_general x1, matrix products, per_device(): jnp.einsum('ack,kn->anc', masked, dft_basis, preferred_element_type=jnp.f...  49.8 us
    dot_general x1, local copies, waits for them, and re-layouts, project(): jnp.einsum('brl,lbn->brn', basis_piece, data_rows, preferred_element_type...  36 us
    dot_general x1, matrix products, project(): jnp.einsum('brl,lbn->brn', basis_piece, data_rows, preferred_element_type...  36 us
    all_to_all x2, local copies, waits for them, and re-layouts, per_device(): lax.all_to_all(part_sums, 'ch', split_axis=0, concat_axis=3, tiled=True)  34.7 us
    convert_element_type x1, local copies, waits for them, and re-layouts, per_device(): (fourier * norm_scale).astype(jnp.bfloat16)  31.3 us
    another operation x1, local copies, waits for them, and re-layouts, per_device(): fourier.reshape(lat_rows, slot_count, 4 * chan_dev)  28.4 us
  transfers between devices with their start and end apart: 2, of which 1 were waited for; matrix products, arithmetic and copies ran while one was open for 20% of the time, Pallas kernels for 0%

commit v1 on v0

--- a/solution.py
+++ b/solution.py
@@ -5,6 +5,30 @@
 from jax.sharding import PartitionSpec as P
 
 NLAT = 721
+
+
+def split_up(x, dim, size):
+    dims = x.shape
+    tiles = x.reshape(*dims[:dim], size, dims[dim] // size, *dims[dim + 1 :])
+    return jnp.moveaxis(tiles, dim, 0)
+
+
+def in_order(blocks, dim):
+    blocks = jnp.moveaxis(blocks, 0, dim)
+    lengths = blocks.shape
+    return blocks.reshape(*lengths[:dim], lengths[dim] * lengths[dim + 1], *lengths[dim + 2 :])
+
+
+def rotated_exchange(x, axis, split_dim, concat_dim):
+    size, mine = (lax.axis_size(axis), lax.axis_index(axis))
+    parts = split_up(x, split_dim, size)
+    result = parts
+    for step in range(1, size):
+        target, source = ((mine + step) % size, (mine - step) % size)
+        sent = lax.dynamic_index_in_dim(parts, target, 0)
+        other = lax.ppermute(sent, axis, [(i, (i + step) % size) for i in range(size)])
+        result = lax.dynamic_update_slice_in_dim(result, other, source, axis=0)
+    return in_order(result, concat_dim)
 
 
 def dft_table(points, modes, lon_count):
@@ -42,13 +66,7 @@
     dft_basis = dft_table(points, orders.reshape(-1), lon_count).reshape(lon_count, 4 * slot_count)
     fourier = jnp.einsum("ack,kn->anc", masked, dft_basis, preferred_element_type=jnp.float32)
     fourier = (fourier * norm_scale).astype(jnp.bfloat16).reshape(lat_rows, slot_count, 4, chan_dev)
-    received = lax.all_to_all(
-        fourier.reshape(lat_rows, slot_count, 4 * chan_dev),
-        "lat",
-        split_axis=1,
-        concat_axis=0,
-        tiled=True,
-    )
+    received = rotated_exchange(fourier.reshape(lat_rows, slot_count, 4 * chan_dev), "lat", 1, 0)
     group_start = lax.axis_index("lat") * group_size
     bound_group = lax.dynamic_slice_in_dim(bound_all, group_start, group_size)
     keep_group = lax.dynamic_slice_in_dim(keep_all, group_start, group_size)

time: 955 us -> 968 us (1.014)
  the two profiles are of different devices: /device:TPU:0 before, /device:TPU:28 now
where the time goes in v1:
time: 968 us; the launch traced here: 963 us
  waiting for transfers between devices  341 us (35%)
  local copies, waits for them, and re-layouts  255 us (26%)
  blocking collectives  209 us (22%)
  matrix products  85.8 us (9%)
  other arithmetic  51.9 us (5%)
  between operations  13.6 us (1%)
    ppermute x7, waiting for transfers between devices, rotated_exchange(): lax.ppermute(sent, axis, [(i, (i + step) % size) for i in range(size)])  340 us
    all_to_all x1, blocking collectives, per_device(): lax.all_to_all(part_sums, 'ch', split_axis=0, concat_axis=3, tiled=True)  209 us
    dot_general x1, matrix products, per_device(): jnp.einsum('ack,kn->anc', masked, dft_basis, preferred_element_type=jnp.f...  49.8 us
    another operation x8, local copies, waits for them, and re-layouts  46.4 us
    dynamic_update_slice x8, local copies, waits for them, and re-layouts, rotated_exchange(): result = lax.dynamic_update_slice_in_dim(result, other, source, axis=0)  45.7 us
    dot_general x1, local copies, waits for them, and re-layouts, project(): jnp.einsum('brl,lbn->brn', basis_piece, data_rows, preferred_element_type...  36 us
    dot_general x1, matrix products, project(): jnp.einsum('brl,lbn->brn', basis_piece, data_rows, preferred_element_type...  36 us
    all_to_all x2, local copies, waits for them, and re-layouts, per_device(): lax.all_to_all(part_sums, 'ch', split_axis=0, concat_axis=3, tiled=True)  34.7 us
  transfers between devices with their start and end apart: 8, of which 5 were waited for; matrix products, arithmetic and copies ran while one was open for 28% of the time, Pallas kernels for 0%

profile of v1, /device:TPU:28, one launch (start us, length us, event | category | flops | bytes accessed | tf_op | source)
XLA Modules:
  0.0 963.4 jit_solution(9368798342510541537)
XLA Ops:
  7.7 19.0 %cosine_convert_fusion = (bf16[1440,768,1]{1,0,2:T(8,128)(2,1)S(1)}, bf16[1440,768,1]{1,0,2:T(8,128)(2,1)S(1)}) fusion(s32[768]{0:T(1024)S(1)} %mul.66), kind=kLoop, calls=%fused_computation.18 | loop fusion | flops 13271040 | bytes 4426752 | tf_op jit(solution)/shard_map/convert
  29.9 13.2 %copy.59 = bf16[1440,768,2]{0,2,1:T(2,128)(2,1)} copy(bf16[1440,768,2]{1,0,2:T(8,128)(2,1)} %pad_maximum_fusion) | data formatting | bytes 8847360 | tf_op jit(solution)/shard_map/stack | solution.py:37
  43.1 10.9 %convert_element_type.30 = bf16[1440,1536]{0,1:T(8,128)(2,1)} reshape(bf16[1440,768,2]{0,2,1:T(2,128)(2,1)} %copy.59) | data formatting | bytes 8847360 | tf_op jit(solution)/shard_map/convert_element_type | solution.py:37
  54.0 16.7 %broadcast_select_fusion = bf16[91,64,1440]{2,1,0:T(8,128)(2,1)} fusion(bf16[91,64,1440]{2,1,0:T(8,128)(2,1)} %param.3, pred[91]{0:T(512)(128)(4,1)S(1)} %add_compare_fusion), kind=kLoop, calls=%fused_computation.10 | loop fusion | flops 8386560 | bytes 33546332 | tf_op jit(solution)/shard_map/jit(_where)/select_n | solution.py:63
  70.8 49.8 %fusion = bf16[91,1536,64]{1,0,2:T(8,128)(2,1)} fusion(bf16[91,64,1440]{2,1,0:T(8,128)(2,1)} %broadcast_select_fusion, bf16[1440,1536]{0,1:T(8,128)(2,1)S(1)} %copy-done.5), kind=kOutput, calls=%fused_computation.1 | convolution fusion | flops 25781403648 | bytes 39088128 | tf_op jit(solution)/shard_map/ack,kn->anc/dot_general | solution.py:67
  120.6 31.4 %copy.62 = bf16[91,1536,64]{0,2,1:T(8,128)(2,1)} copy(bf16[91,1536,64]{1,0,2:T(8,128)(2,1)} %fusion) | data formatting | bytes 35782656 | tf_op jit(solution)/shard_map/convert_element_type | solution.py:68
  151.9 14.5 %constant_dynamic-slice_fusion = (bf16[91,1,48,256]{0,3,2,1:T(8,128)(2,1)S(1)}, bf16[91,1,48,256]{0,3,2,1:T(8,128)(2,1)}, bf16[91,1,48,256]{0,3,2,1:T(8,128)(2,1...) fusion(bf16[91,8,48,256]{0,3,2,1:T(8,128)(2,1)} %bitcast.38, ...), kind=kLoop, calls=%fused_computation.25 | loop fusion | bytes 31309852 | tf_op jit(solution)/shard_map/dynamic-slice.6
  166.4 4.9 copy.63
  171.3 4.8 copy.65
  177.9 4.9 copy.67
  184.4 4.8 copy.69
  196.9 4.7 copy.73
  204.7 17.3 %collective-permute-done = bf16[1,91,48,256]{3,2,1,0:T(8,128)(2,1)} collective-permute-done((bf16[1,91,48,256]{3,2,1,0:T(8,128)(2,1)}, bf16[1,91,48,256]{3,2,1,0:T(8,128)(2,1)}, u32[]{:S(2)}, u32[]{:S(2)}) %collective-permute-start) | collective-permute-done | bytes 2236448 | tf_op jit(solution)/shard_map/ppermute | solution.py:29
  222.6 47.6 %collective-permute-done.1 = bf16[1,91,48,256]{3,2,1,0:T(8,128)(2,1)} collective-permute-done((bf16[1,91,48,256]{3,2,1,0:T(8,128)(2,1)}, bf16[1,91,48,256]{3,2,1,0:T(8,128)(2,1)}, u32[]{:S(2)}, u32[]{:S(2)}) %collective-permute-start.1) | collective-permute-done | bytes 2236448 | tf_op jit(solution)/shard_map/ppermute | solution.py:29
  278.7 38.0 %collective-permute-done.2 = bf16[1,91,48,256]{3,2,1,0:T(8,128)(2,1)} collective-permute-done((bf16[1,91,48,256]{3,2,1,0:T(8,128)(2,1)}, bf16[1,91,48,256]{3,2,1,0:T(8,128)(2,1)}, u32[]{:S(2)}, u32[]{:S(2)}) %collective-permute-start.2) | collective-permute-done | bytes 2236448 | tf_op jit(solution)/shard_map/ppermute | solution.py:29
  321.4 236.0 %collective-permute-done.3 = bf16[1,91,48,256]{3,2,1,0:T(8,128)(2,1)} collective-permute-done((bf16[1,91,48,256]{3,2,1,0:T(8,128)(2,1)}, bf16[1,91,48,256]{3,2,1,0:T(8,128)(2,1)}, u32[]{:S(2)}, u32[]{:S(2)}) %collective-permute-start.3) | collective-permute-done | bytes 2236448 | tf_op jit(solution)/shard_map/ppermute | solution.py:29
  572.7 4.7 copy.76
  598.5 29.8 %copy.77 = bf16[8,91,48,256]{3,2,1,0:T(8,128)(2,1)} copy(bf16[8,91,48,256]{1,3,2,0:T(8,128)(2,1)} %constant_dynamic-update-slice_fusion) | data formatting | bytes 35782656 | tf_op jit(solution)/shard_map/dynamic_update_slice | solution.py:30
  628.4 36.0 %fusion.9 = f32[48,721,256]{2,1,0:T(8,128)} fusion(bf16[48,721,728]{2,1,0:T(8,128)(2,1)} %all-gather.2.cloned.1.call-done, bf16[728,48,256]{2,1,0:T(8,128)(2,1)} %bitcast.43), kind=kOutput, calls=%fused_computation.11 | convolution fusion | flops 12899647488 | bytes 103719168 | tf_op jit(solution)/shard_map/brl,lbn->brn/dot_general | solution.py:41
  664.3 36.0 %copy.79 = f32[48,721,256]{1,2,0:T(8,128)} copy(f32[48,721,256]{2,1,0:T(8,128)} %fusion.9) | data formatting | bytes 70877184 | tf_op jit(solution)/shard_map/brl,lbn->brn/dot_general | solution.py:41
  700.4 12.8 %fusion.2 = f32[48,721,2,64]{1,3,2,0:T(8,128)S(1)} fusion(f32[48,721,2,2,64]{1,4,3,2,0:T(8,128)} %bitcast.40, f32[48]{0:T(128)S(1)} %dynamic-slice_convert_fusion, pred[48,721]{1,0:T(8,128)(4,1)S(1)} %iota_compare_fusion), kind=kLoop, calls=%fused_computation.4 | loop fusion | flops 8859648 | bytes 53192688 | tf_op jit(solution)/shard_map/mul | solution.py:49
  713.2 208.6 %all_to_all.18 = f32[48,721,2,64]{1,3,2,0:T(8,128)S(1)} all-to-all(f32[48,721,2,64]{1,3,2,0:T(8,128)S(1)} %fusion.2), channel_id=1, replica_groups=mesh['lat'=8,'ch'=4] {'ch'}, dimensions={0} | all-to-all | bytes 35438592 | tf_op jit(solution)/shard_map/all_to_all | solution.py:76
  921.9 6.9 copy.81
  928.8 27.7 %copy.82 = f32[12,721,2,256]{3,2,1,0:T(2,128)} copy(f32[12,721,2,256]{1,3,2,0:T(8,128)} %bitcast.42) | data formatting | bytes 35438592 | tf_op jit(solution)/shard_map/all_to_all | solution.py:76
  (54 shorter events, 68.6 us)
Async XLA Ops:
  6.5 0.8 copy-start.6
  6.5 621.8 %all-gather.2.cloned.1.call-start = ((), (), s32[]{:S(2)}) async-start(), calls=%async_computation.1 | async-start | bytes 67092480 | tf_op jit(solution)/shard_map/all_gather | solution.py:74
  54.0 16.7 %copy-start.5 = (bf16[1440,1536]{0,1:T(8,128)(2,1)S(1)}, bf16[1440,1536]{0,1:T(8,128)(2,1)}, u32[]{:S(2)}) copy-start(bf16[1440,1536]{0,1:T(8,128)(2,1)} %convert_element_type.30) | copy-start | bytes 13271044
  171.3 50.7 %collective-permute-start = (bf16[1,91,48,256]{3,2,1,0:T(8,128)(2,1)}, bf16[1,91,48,256]{3,2,1,0:T(8,128)(2,1)}, u32[]{:S(2)}, u32[]{:S(2)}) collective-permute-start(bf16[1,91,48,256]{3,2,1,0:T(8,128)(2,1)} %bitcast.50), channel_id=1, source_target_pairs={{0,4},{4,8},{8,12},{12,16},{16,20},{20,24},{24,28},{28,0},{1,5},{5... | collective-permute-start | bytes 6709256 | tf_op jit(solution)/shard_map/ppermute | solution.py:29
  176.2 94.1 %collective-permute-start.1 = (bf16[1,91,48,256]{3,2,1,0:T(8,128)(2,1)}, bf16[1,91,48,256]{3,2,1,0:T(8,128)(2,1)}, u32[]{:S(2)}, u32[]{:S(2)}) collective-permute-start(bf16[1,91,48,256]{3,2,1,0:T(8,128)(2,1)} %bitcast.49), channel_id=1, source_target_pairs={{0,8},{4,12},{8,16},{12,20},{16,24},{20,28},{24,0},{28,4},{1,9},{5... | collective-permute-start | bytes 6709256 | tf_op jit(solution)/shard_map/ppermute | solution.py:29
  182.8 133.9 %collective-permute-start.2 = (bf16[1,91,48,256]{3,2,1,0:T(8,128)(2,1)}, bf16[1,91,48,256]{3,2,1,0:T(8,128)(2,1)}, u32[]{:S(2)}, u32[]{:S(2)}) collective-permute-start(bf16[1,91,48,256]{3,2,1,0:T(8,128)(2,1)} %bitcast.45), channel_id=1, source_target_pairs={{0,12},{4,16},{8,20},{12,24},{16,28},{20,0},{24,4},{28,8},{1,13},{... | collective-permute-start | bytes 6709256 | tf_op jit(solution)/shard_map/ppermute | solution.py:29
  189.2 368.1 %collective-permute-start.3 = (bf16[1,91,48,256]{3,2,1,0:T(8,128)(2,1)}, bf16[1,91,48,256]{3,2,1,0:T(8,128)(2,1)}, u32[]{:S(2)}, u32[]{:S(2)}) collective-permute-start(bf16[1,91,48,256]{3,2,1,0:T(8,128)(2,1)} %bitcast.46), channel_id=1, source_target_pairs={{0,16},{4,20},{8,24},{12,28},{16,0},{20,4},{24,8},{28,12},{1,17},{... | collective-permute-start | bytes 6709256 | tf_op jit(solution)/shard_map/ppermute | solution.py:29
  195.1 368.3 %collective-permute-start.4 = (bf16[1,91,48,256]{3,2,1,0:T(8,128)(2,1)}, bf16[1,91,48,256]{3,2,1,0:T(8,128)(2,1)}, u32[]{:S(2)}, u32[]{:S(2)}) collective-permute-start(bf16[1,91,48,256]{3,2,1,0:T(8,128)(2,1)} %bitcast.47), channel_id=1, source_target_pairs={{0,20},{4,24},{8,28},{12,0},{16,4},{20,8},{24,12},{28,16},{1,21},{... | collective-permute-start | bytes 6709256 | tf_op jit(solution)/shard_map/ppermute | solution.py:29
  222.0 346.1 %collective-permute-start.5 = (bf16[1,91,48,256]{3,2,1,0:T(8,128)(2,1)}, bf16[1,91,48,256]{3,2,1,0:T(8,128)(2,1)}, u32[]{:S(2)}, u32[]{:S(2)}) collective-permute-start(bf16[1,91,48,256]{3,2,1,0:T(8,128)(2,1)} %bitcast.48), channel_id=1, source_target_pairs={{0,24},{4,28},{8,0},{12,4},{16,8},{20,12},{24,16},{28,20},{1,25},{... | collective-permute-start | bytes 6709256 | tf_op jit(solution)/shard_map/ppermute | solution.py:29
  270.2 302.5 %collective-permute-start.6 = (bf16[1,91,48,256]{3,2,1,0:T(8,128)(2,1)}, bf16[1,91,48,256]{3,2,1,0:T(8,128)(2,1)}, u32[]{:S(2)}, u32[]{:S(2)}) collective-permute-start(bf16[1,91,48,256]{3,2,1,0:T(8,128)(2,1)} %bitcast.44), channel_id=1, source_target_pairs={{0,28},{4,0},{8,4},{12,8},{16,12},{20,16},{24,20},{28,24},{1,29},{... | collective-permute-start | bytes 6709256 | tf_op jit(solution)/shard_map/ppermute | solution.py:29
  581.4 3.0 copy-start
  584.4 3.0 copy-start.1
  587.4 3.0 copy-start.2
  590.5 3.0 copy-start.3
  593.5 3.0 copy-start.4
Sparse Core Ops, SparseCore 0:
  8.9 319.0 all-gather.1
